TPU v7x, 32 devices: a whole 2x2x4 slice. The times are simulated.
32 devices in a mesh: groups: 2 (over y), seq: 4 (over z), batch: 2 (over x), head: 2 (over core).
Axes of the slice: x: 2, y: 2, z: 4, core: 2. Of those that a mesh axis runs over, the one named last changes fastest.
Arguments:
- queries: bfloat16 [64, 64, 128], P(('groups', 'seq', 'batch'), 'head'), parts along dimension 0, may hold values from -16 to 16
- fresh_token_keys: bfloat16 [64, 8, 128], P(('groups', 'seq', 'batch'), 'head'), parts along dimension 0, may hold values from -12 to 12
- fresh_token_values: bfloat16 [64, 8, 128], P(('groups', 'seq', 'batch'), 'head'), parts along dimension 0, may hold values from -6 to 6
- shared_prefix_keys: bfloat16 [16384, 8, 128], P(('groups', 'seq'), 'head'), parts along dimension 0, may hold values from -6 to 6
- shared_prefix_values: bfloat16 [16384, 8, 128], P(('groups', 'seq'), 'head'), parts along dimension 0, may hold values from -6 to 6
- sequence_suffix_keys: bfloat16 [64, 192, 8, 128], P(('groups', 'seq', 'batch'), None, 'head'), parts along dimension 0, may hold values from -8 to 8
- sequence_suffix_values: bfloat16 [64, 192, 8, 128], P(('groups', 'seq', 'batch'), None, 'head'), parts along dimension 0, may hold values from -6 to 6
- suffix_lengths: int32 [64], P(('groups', 'seq', 'batch')), parts along dimension 0, may hold values from 0 to 192, as said below
Outputs:
- context: bfloat16 [64, 64, 128], P(('groups', 'seq', 'batch'), 'head'), parts along dimension 0
There are 2 independent parts, one for each index of `groups`. A program takes and returns all parts, laid end to end along the dimension named above; each array names one. Nothing has to cross between parts.
Inputs may be any that keep to these rules, and one draw needn't show every extreme that they name: `suffix_lengths`: slots at and beyond a sequence's length hold no token. Some sequence has all 192 slots live in every draw.
All inputs are finite; a program needn't handle non-finite values.
Results may differ from a plain program's by a relative error of at most 0.002.
Values may be sent and summed in bfloat16 or wider, within the bound.
A program may use at most 64 MiB of HBM per device.

v0:
```python
import math
import jax
import jax.numpy as jnp
from jax import lax
from jax.sharding import PartitionSpec as P


def prefix_block(query_rows, block_keys, block_values, inv_root):
    scores = (
        lax.dot_general(
            query_rows, block_keys, (((1,), (1,)), ((), ())), preferred_element_type=jnp.float32
        )
        * inv_root
    )
    maxima = jnp.max(scores, axis=1)
    weights = jnp.exp(scores - maxima[:, None]).astype(jnp.bfloat16)
    totals = jnp.sum(weights, axis=1, dtype=jnp.float32)
    outputs = jnp.dot(weights, block_values, preferred_element_type=jnp.float32)
    return (maxima, totals, outputs)


def body(
    queries,
    fresh_token_keys,
    fresh_token_values,
    shared_prefix_keys,
    shared_prefix_values,
    sequence_suffix_keys,
    sequence_suffix_values,
    suffix_lengths,
):
    own_count, head_count, width = queries.shape
    kv_count = shared_prefix_keys.shape[1]
    query_group = head_count // kv_count
    inv_root = 1.0 / math.sqrt(width)
    seq_count = lax.axis_size("seq")
    gathered = lax.all_gather(queries, "seq", axis=0, tiled=True)
    row_count = gathered.shape[0]
    grouped = gathered.reshape(row_count, kv_count, query_group, width)
    maxima_list = []
    totals_list = []
    outputs_list = []
    for kv_head in range(kv_count):
        query_rows = grouped[:, kv_head].reshape(row_count * query_group, width)
        maxima, totals, outputs = prefix_block(
            query_rows, shared_prefix_keys[:, kv_head], shared_prefix_values[:, kv_head], inv_root
        )
        maxima_list.append(maxima.reshape(row_count, query_group))
        totals_list.append(totals.reshape(row_count, query_group))
        outputs_list.append(outputs.reshape(row_count, query_group, width))
    block_max = jnp.stack(maxima_list, axis=1).reshape(row_count, head_count)
    block_total = jnp.stack(totals_list, axis=1).reshape(row_count, head_count)
    block_out = jnp.stack(outputs_list, axis=1).reshape(row_count, head_count, width)
    own_rows = queries.reshape(own_count, kv_count, query_group, width)
    own_scores = (
        jnp.einsum("bgqd,bgd->bgq", own_rows, fresh_token_keys, preferred_element_type=jnp.float32)
        * inv_root
    )
    recent = (
        jnp.einsum(
            "bgqd,bsgd->bgqs", own_rows, sequence_suffix_keys, preferred_element_type=jnp.float32
        )
        * inv_root
    )
    slot_count = sequence_suffix_keys.shape[1]
    live = (jnp.arange(slot_count, dtype=jnp.int32)[None, :] < suffix_lengths[:, None])[
        :, None, None, :
    ]
    local_max = jnp.maximum(
        own_scores, jnp.max(jnp.where(live, recent, own_scores[..., None]), axis=-1)
    )
    recent_weights = jnp.where(
        live, jnp.exp(jnp.where(live, recent - local_max[..., None], 0.0)), 0.0
    ).astype(jnp.bfloat16)
    own_weights = jnp.exp(own_scores - local_max).astype(jnp.bfloat16)
    local_total = jnp.sum(recent_weights, axis=-1, dtype=jnp.float32) + own_weights.astype(
        jnp.float32
    )
    local_out = jnp.einsum(
        "bgqs,bsgd->bgqd",
        recent_weights,
        sequence_suffix_values,
        preferred_element_type=jnp.float32,
    )
    local_out = (
        local_out
        + own_weights.astype(jnp.float32)[..., None]
        * fresh_token_values.astype(jnp.float32)[:, :, None, :]
    )
    local_max = local_max.reshape(own_count, head_count)
    local_total = local_total.reshape(own_count, head_count)
    local_out = local_out.reshape(own_count, head_count, width)
    state_shape = (seq_count, own_count, head_count)
    got_out, got_max, got_total = (
        lax.all_to_all(
            block_out.reshape(seq_count, own_count, head_count, width),
            "seq",
            split_axis=0,
            concat_axis=0,
            tiled=True,
        ),
        lax.all_to_all(
            block_max.reshape(state_shape), "seq", split_axis=0, concat_axis=0, tiled=True
        ),
        lax.all_to_all(
            block_total.reshape(state_shape), "seq", split_axis=0, concat_axis=0, tiled=True
        ),
    )
    highest = jnp.maximum(local_max, jnp.max(got_max, axis=0))
    block_scale = jnp.exp(got_max - highest[None])
    local_scale = jnp.exp(local_max - highest)
    total = local_total * local_scale + jnp.sum(got_total * block_scale, axis=0)
    numerator = local_out * local_scale[..., None] + jnp.sum(
        got_out * block_scale[..., None], axis=0
    )
    return (numerator / total[..., None]).astype(jnp.bfloat16)


def solution(mesh):
    in_specs = (
        P(("groups", "seq", "batch"), "head", None),
        P(("groups", "seq", "batch"), "head", None),
        P(("groups", "seq", "batch"), "head", None),
        P(("groups", "seq"), "head", None),
        P(("groups", "seq"), "head", None),
        P(("groups", "seq", "batch"), None, "head", None),
        P(("groups", "seq", "batch"), None, "head", None),
        P(("groups", "seq", "batch")),
    )
    out_specs = P(("groups", "seq", "batch"), "head", None)
    return jax.shard_map(body, mesh=mesh, in_specs=in_specs, out_specs=out_specs, check_vma=False)
```

profile of v0, /device:TPU:0, one launch (start us, length us, event | category | flops | bytes accessed | tf_op | source)
XLA Modules:
  0.0 72.7 jit_solution(282723957632736956)
XLA Ops:
  0.0 8.9 %fusion.19 = (bf16[2048,1,128]{2,1,0:T(2,128)(2,1)S(1)}, bf16[2048,1,128]{2,1,0:T(2,128)(2,1)}, bf16[2048,1,128]{2,1,0:T(2,128)(2,1)}, bf16[2048,1,128]{2,1,0:T(2,128)(2,1)}) fusion(bf16[2048,4,128]{2,1,0:T(4,128)(2,1)} %param.11), kind=kLoop, calls=%fused_computation.62 | loop fusion | bytes 4194304 | tf_op jit(solution)/shard_map/slice | solution.py:46
  8.9 15.1 %all_gather.3 = bf16[16,32,128]{2,1,0:T(8,128)(2,1)S(1)} all-gather(bf16[4,32,128]{2,1,0:T(8,128)(2,1)S(1)} %copy-done.5), channel_id=1, replica_groups=mesh['groups'=2,'seq'=4,'batch'=2,'head'=2] {'seq'}, dimensions={0}, use_global_device_ids=true | all-gather | bytes 163840 | tf_op jit(solution)/shard_map/all_gather | solution.py:37
  24.0 0.4 fusion.24
  24.4 0.3 convert_reduce_fusion.3
  24.8 1.6 %fusion.23 = (f32[128]{0:T(128)S(1)}, f32[128,2048]{1,0:T(8,128)S(1)}) fusion(bf16[2048,1,128]{2,1,0:T(2,128)(2,1)} %get-tuple-element.13, bf16[16,4,8,128]{3,2,1,0:T(8,128)(2,1)S(1)} %bitcast.99), kind=kOutput, calls=%fused_computation.66 | convolution fusion | flops 67633024 | bytes 1606144 | tf_op jit(solution)/shard_map/dot_general | solution.py:10
  26.4 0.3 convert_reduce_fusion.2
  26.8 1.6 %fusion.22 = (f32[128]{0:T(128)S(1)}, f32[128,2048]{1,0:T(8,128)S(1)}) fusion(bf16[2048,1,128]{2,1,0:T(2,128)(2,1)} %get-tuple-element.12, bf16[16,4,8,128]{3,2,1,0:T(8,128)(2,1)S(1)} %bitcast.100), kind=kOutput, calls=%fused_computation.65 | convolution fusion | flops 67633024 | bytes 1606144 | tf_op jit(solution)/shard_map/dot_general | solution.py:10
  28.4 1.0 %copy-done.1 = f32[128,2048]{1,0:T(8,128)} copy-done((f32[128,2048]{1,0:T(8,128)}, f32[128,2048]{1,0:T(8,128)S(1)}, u32[]{:S(2)}) %copy-start.1) | copy-done | bytes 1048600
  29.5 0.3 convert_reduce_fusion.1
  29.8 1.6 %fusion.21 = (f32[128]{0:T(128)S(1)}, f32[128,2048]{1,0:T(8,128)S(1)}) fusion(bf16[2048,1,128]{2,1,0:T(2,128)(2,1)} %get-tuple-element.14, bf16[16,4,8,128]{3,2,1,0:T(8,128)(2,1)S(1)} %bitcast.101), kind=kOutput, calls=%fused_computation.64 | convolution fusion | flops 67633024 | bytes 1606144 | tf_op jit(solution)/shard_map/dot_general | solution.py:10
  31.5 1.0 %copy-done.3 = f32[128,2048]{1,0:T(8,128)} copy-done((f32[128,2048]{1,0:T(8,128)}, f32[128,2048]{1,0:T(8,128)S(1)}, u32[]{:S(2)}) %copy-start.3) | copy-done | bytes 1048600
  32.5 0.3 convert_reduce_fusion
  33.0 0.7 reshape.116
  33.6 5.0 %all-to-all-start.2 = ((f32[4,1,128]{2,1,0:T(1,128)}), f32[4,1,128]{2,1,0:T(1,128)S(1)}, u32[]{:S(2)}, u32[]{:S(2)}) async-start(f32[4,1,128]{2,1,0:T(1,128)} %reshape.116), calls=%async_computation.2 | async-start | bytes 4096 | tf_op jit(solution)/shard_map/all_to_all | solution.py:105
  39.2 0.6 select_reduce_fusion
  39.8 0.2 convert_reduce_fusion.4
  40.0 8.1 %fusion.20 = (bf16[2048,1,128]{2,1,0:T(2,128)(2,1)S(1)}, bf16[2048,1,128]{2,1,0:T(2,128)(2,1)S(1)}, bf16[2048,1,128]{2,1,0:T(2,128)(2,1)S(1)}, bf16[2048,1,128]{2,1,0:T(2,128)(2,1)S(1)}) fusion(bf16[2048,4,128]{2,1,0:T(4,128)(2,1)} %param.12), kind=kLoop, calls=%fused_computation.63 | loop fusion | bytes 4194304 | tf_op jit(solution)/shard_map/slice | solution.py:46
  48.2 0.4 convolution_bitcast_fusion.3
  48.5 0.4 convolution_bitcast_fusion.2
  48.9 0.5 copy-done.2
  49.4 0.4 convolution_bitcast_fusion.1
  49.7 0.4 convolution_bitcast_fusion
  50.2 0.7 reshape.114
  50.9 5.1 %all-to-all-start = ((f32[4,1,128]{2,1,0:T(1,128)}), f32[4,1,128]{2,1,0:T(1,128)S(1)}, u32[]{:S(2)}, u32[]{:S(2)}) async-start(f32[4,1,128]{2,1,0:T(1,128)} %reshape.114), calls=%async_computation | async-start | bytes 4096 | tf_op jit(solution)/shard_map/all_to_all | solution.py:102
  56.2 0.7 copy.39
  56.9 0.5 broadcast.26
  57.4 0.7 reduce
  58.2 3.2 %all-to-all-done = f32[4,1,128]{2,1,0:T(1,128)S(1)} async-done(((f32[4,1,128]{2,1,0:T(1,128)}), f32[4,1,128]{2,1,0:T(1,128)S(1)}, u32[]{:S(2)}, u32[]{:S(2)}) %all-to-all-start) | async-done | bytes 2080 | tf_op jit(solution)/shard_map/all_to_all | solution.py:102
  61.4 3.4 %all-to-all-start.1 = ((f32[4,4,32,128]{3,2,1,0:T(8,128)}), f32[4,4,32,128]{3,2,1,0:T(8,128)S(1)}, u32[]{:S(2)}, u32[]{:S(2)}) async-start(f32[4,4,32,128]{3,2,1,0:T(8,128)} %bitcast.30), calls=%async_computation.1 | async-start | bytes 524288 | tf_op jit(solution)/shard_map/all_to_all | solution.py:95
  64.8 0.7 reduce.1
  65.6 5.9 %all-to-all-done.1 = f32[4,4,32,128]{3,2,1,0:T(8,128)S(1)} async-done(((f32[4,4,32,128]{3,2,1,0:T(8,128)}), f32[4,4,32,128]{3,2,1,0:T(8,128)S(1)}, u32[]{:S(2)}, u32[]{:S(2)}) %all-to-all-start.1) | async-done | bytes 262176 | tf_op jit(solution)/shard_map/all_to_all | solution.py:95
  71.7 1.0 %fusion.4 = bf16[4,32,128]{2,1,0:T(8,128)(2,1)} fusion(f32[4,32,128]{2,1,0:T(8,128)S(1)} %multiply_reduce_fusion, bf16[4,192,4,128]{3,2,1,0:T(4,128)(2,1)S(1)} %copy-done.7, f32[4,32]{1,0:T(4,128)S(1)} %get-tuple-element.5, f32[4,32]{1,0:T(4,128)S(1)} %get-tuple-element.6, f32[4,4,128]{2,1,0:T(4,128)S(1)} %convert_element_type.46, ...), kind=kOutput, calls=%fused_computation.14 | convolution fusion | flops 6488064 | bytes 994048 | tf_op jit(solution)/shard_map/bgqs,bsgd->bgqd/dot_general | solution.py:79
  (48 shorter events, 1.7 us)
Async XLA Ops:
  0.0 39.2 %copy-start = (bf16[4,192,4,128]{3,2,1,0:T(4,128)(2,1)S(1)}, bf16[4,192,4,128]{3,2,1,0:T(4,128)(2,1)}, u32[]{:S(2)}) copy-start(bf16[4,192,4,128]{3,2,1,0:T(4,128)(2,1)} %param.13) | copy-start | bytes 2359300
  0.0 8.9 %copy-start.5 = (bf16[4,32,128]{2,1,0:T(8,128)(2,1)S(1)}, bf16[4,32,128]{2,1,0:T(8,128)(2,1)}, u32[]{:S(2)}) copy-start(bf16[4,32,128]{2,1,0:T(8,128)(2,1)} %param.8) | copy-start | bytes 98308
  28.4 1.0 %copy-start.1 = (f32[128,2048]{1,0:T(8,128)}, f32[128,2048]{1,0:T(8,128)S(1)}, u32[]{:S(2)}) copy-start(f32[128,2048]{1,0:T(8,128)S(1)} %get-tuple-element.22) | copy-start | bytes 3145732
  28.4 10.5 %copy-start.8 = (bf16[4,4,128]{2,1,0:T(4,128)(2,1)S(1)}, bf16[4,4,128]{2,1,0:T(4,128)(2,1)}, u32[]{:S(2)}) copy-start(bf16[4,4,128]{2,1,0:T(4,128)(2,1)} %param.9) | copy-start | bytes 12292
  28.4 10.7 %copy-start.9 = (s32[4]{0:T(128)S(1)}, s32[4]{0:T(128)}, u32[]{:S(2)}) copy-start(s32[4]{0:T(128)} %param.15) | copy-start | bytes 52
  31.5 1.0 %copy-start.3 = (f32[128,2048]{1,0:T(8,128)}, f32[128,2048]{1,0:T(8,128)S(1)}, u32[]{:S(2)}) copy-start(f32[128,2048]{1,0:T(8,128)S(1)} %get-tuple-element.20) | copy-start | bytes 3145732
  33.6 17.3 %all-to-all-start.2 = ((f32[4,1,128]{2,1,0:T(1,128)}), f32[4,1,128]{2,1,0:T(1,128)S(1)}, u32[]{:S(2)}, u32[]{:S(2)}) async-start(f32[4,1,128]{2,1,0:T(1,128)} %reshape.116), calls=%async_computation.2 | async-start | bytes 4096 | tf_op jit(solution)/shard_map/all_to_all | solution.py:105
  48.1 1.2 %copy-start.2 = (f32[128,2048]{1,0:T(8,128)S(1)}, f32[128,2048]{1,0:T(8,128)}, u32[]{:S(2)}) copy-start(f32[128,2048]{1,0:T(8,128)} %copy-done.1) | copy-start | bytes 3145732
  48.1 1.6 %copy-start.4 = (f32[128,2048]{1,0:T(8,128)S(1)}, f32[128,2048]{1,0:T(8,128)}, u32[]{:S(2)}) copy-start(f32[128,2048]{1,0:T(8,128)} %copy-done.3) | copy-start | bytes 3145732
  49.4 7.5 %copy-start.6 = (bf16[4,4,128]{2,1,0:T(4,128)(2,1)S(1)}, bf16[4,4,128]{2,1,0:T(4,128)(2,1)}, u32[]{:S(2)}) copy-start(bf16[4,4,128]{2,1,0:T(4,128)(2,1)} %param.10) | copy-start | bytes 12292
  49.7 22.0 %copy-start.7 = (bf16[4,192,4,128]{3,2,1,0:T(4,128)(2,1)S(1)}, bf16[4,192,4,128]{3,2,1,0:T(4,128)(2,1)}, u32[]{:S(2)}) copy-start(bf16[4,192,4,128]{3,2,1,0:T(4,128)(2,1)} %param.14) | copy-start | bytes 2359300
  50.9 10.5 %all-to-all-start = ((f32[4,1,128]{2,1,0:T(1,128)}), f32[4,1,128]{2,1,0:T(1,128)S(1)}, u32[]{:S(2)}, u32[]{:S(2)}) async-start(f32[4,1,128]{2,1,0:T(1,128)} %reshape.114), calls=%async_computation | async-start | bytes 4096 | tf_op jit(solution)/shard_map/all_to_all | solution.py:102
  61.4 10.2 %all-to-all-start.1 = ((f32[4,4,32,128]{3,2,1,0:T(8,128)}), f32[4,4,32,128]{3,2,1,0:T(8,128)S(1)}, u32[]{:S(2)}, u32[]{:S(2)}) async-start(f32[4,4,32,128]{3,2,1,0:T(8,128)} %bitcast.30), calls=%async_computation.1 | async-start | bytes 524288 | tf_op jit(solution)/shard_map/all_to_all | solution.py:95
where the time goes:
time: 73.2 us; the launch traced here: 72.7 us
  local copies, waits for them, and re-layouts  23.3 us (32%)
  blocking collectives  15.1 us (21%)
  starting transfers between devices  13.5 us (18%)
  waiting for transfers between devices  9.17 us (13%)
  matrix products  8.4 us (11%)
  other arithmetic  3.07 us (4%)
    all_gather x1, blocking collectives, body(): gathered = lax.all_gather(queries, 'seq', axis=0, tiled=True)  15.1 us
    slice x1, local copies, waits for them, and re-layouts, body(): shared_prefix_keys[:, kv_head]  8.92 us
    slice x1, local copies, waits for them, and re-layouts, body(): shared_prefix_values[:, kv_head]  8.1 us
    all_to_all x1, waiting for transfers between devices, body(): lax.all_to_all(block_out.reshape(seq_count, own_count, head_count, width)...  5.93 us
    dot_general x4, matrix products, prefix_block(): lax.dot_general(query_rows, block_keys, (((1,), (1,)), ((), ())), preferr...  5.26 us
    all_to_all x1, starting transfers between devices, body(): lax.all_to_all(block_max.reshape(state_shape), 'seq', split_axis=0, conca...  5.09 us
    all_to_all x1, starting transfers between devices, body(): lax.all_to_all(block_total.reshape(state_shape), 'seq', split_axis=0, con...  4.97 us
    unnamed x24, local copies, waits for them, and re-layouts  4.02 us
  transfers between devices with their start and end apart: 3, of which 2 were waited for; matrix products, arithmetic and copies ran while one was open for 20% of the time, Pallas kernels for 0%

commit v1 on v0

--- a/solution.py
+++ b/solution.py
@@ -34,7 +34,9 @@
     query_group = head_count // kv_count
     inv_root = 1.0 / math.sqrt(width)
     seq_count = lax.axis_size("seq")
-    gathered = lax.all_gather(queries, "seq", axis=0, tiled=True)
+    gathered = jnp.concatenate(
+        lax.all_to_all(jnp.stack([queries] * lax.axis_size("seq")), "seq", 0, 0), axis=0
+    )
     row_count = gathered.shape[0]
     grouped = gathered.reshape(row_count, kv_count, query_group, width)
     maxima_list = []

time: 73.2 us -> 68.7 us (0.939)
  blocking collectives: 15.1 us -> 0 us
  starting transfers between devices: 13.5 us -> 19.3 us
  matrix products: 8.4 us -> 14.1 us
  local copies, waits for them, and re-layouts: 23.3 us -> 18.9 us
  other arithmetic: 3.07 us -> 5.54 us
  waiting for transfers between devices: 9.17 us -> 9.95 us
    all_gather x1 -> x0, blocking collectives: 15.1 us -> none  [body(): gathered = lax.all_gather(queries, 'seq', axis=0, tiled=True)]
    all_to_all x0 -> x1, starting transfers between devices: none -> 6.35 us  [body(): lax.all_to_all(jnp.stack([queries] * lax.axis_size('seq')), 'seq', 0, 0)]
    slice x1, local copies, waits for them, and re-layouts: 8.1 us -> 4.46 us  [body(): shared_prefix_values[:, kv_head]]
    dot_general x4, matrix products: 5.26 us -> 8.35 us  [prefix_block(): lax.dot_general(query_rows, block_keys, (((1,), (1,)), ((), ())), preferr...]
    dot_general x4, matrix products: 1.43 us -> 4 us  [prefix_block(): outputs = jnp.dot(weights, block_values, preferred_element_type=jnp.float32)]
    reduce_sum x4, other arithmetic: 1.19 us -> 3.68 us  [prefix_block(): totals = jnp.sum(weights, axis=1, dtype=jnp.float32)]
    unnamed x24 -> x26, local copies, waits for them, and re-layouts: 4.02 us -> 1.55 us
    another operation x0 -> x1, local copies, waits for them, and re-layouts: none -> 1.5 us  [body(): jnp.stack([queries] * lax.axis_size('seq'))]
  transfers between devices with their start and end apart: 3 -> 4, of which waited for: 2 -> 3; matrix products, arithmetic and copies ran while one was open for 20% -> 33% of each run, Pallas kernels for 0% -> 0%
where the time goes in v1:
time: 68.7 us; the launch traced here: 68.1 us
  starting transfers between devices  19.3 us (28%)
  local copies, waits for them, and re-layouts  18.9 us (28%)
  matrix products  14.1 us (21%)
  waiting for transfers between devices  9.95 us (14%)
  other arithmetic  5.54 us (8%)
    slice x1, local copies, waits for them, and re-layouts, body(): shared_prefix_keys[:, kv_head]  9.15 us
    dot_general x4, matrix products, prefix_block(): lax.dot_general(query_rows, block_keys, (((1,), (1,)), ((), ())), preferr...  8.35 us
    all_to_all x1, starting transfers between devices, body(): lax.all_to_all(jnp.stack([queries] * lax.axis_size('seq')), 'seq', 0, 0)  6.35 us
    all_to_all x1, waiting for transfers between devices, body(): lax.all_to_all(block_out.reshape(seq_count, own_count, head_count, width)...  5.93 us
    all_to_all x1, starting transfers between devices, body(): lax.all_to_all(block_total.reshape(state_shape), 'seq', split_axis=0, con...  5.08 us
    all_to_all x1, starting transfers between devices, body(): lax.all_to_all(block_max.reshape(state_shape), 'seq', split_axis=0, conca...  4.49 us
    slice x1, local copies, waits for them, and re-layouts, body(): shared_prefix_values[:, kv_head]  4.46 us
    dot_general x4, matrix products, prefix_block(): outputs = jnp.dot(weights, block_values, preferred_element_type=jnp.float32)  4 us
  transfers between devices with their start and end apart: 4, of which 3 were waited for; matrix products, arithmetic and copies ran while one was open for 33% of the time, Pallas kernels for 0%

profile of v1, /device:TPU:0, one launch (start us, length us, event | category | flops | bytes accessed | tf_op | source)
XLA Modules:
  0.0 68.1 jit_solution(2832082392285049380)
XLA Ops:
  0.0 1.5 %stack.16 = bf16[4,4,32,128]{3,2,1,0:T(8,128)(2,1)} broadcast(bf16[4,32,128]{2,1,0:T(8,128)(2,1)} %param.8), dimensions={1,2,3} | broadcast | bytes 163840 | tf_op jit(solution)/shard_map/stack | solution.py:38
  1.5 6.3 %all-to-all-start = ((bf16[4,4,32,128]{3,2,1,0:T(8,128)(2,1)}), bf16[4,4,32,128]{3,2,1,0:T(8,128)(2,1)S(1)}, u32[]{:S(2)}, u32[]{:S(2)}) async-start(bf16[4,4,32,128]{3,2,1,0:T(8,128)(2,1)} %stack.16), calls=%async_computation | async-start | bytes 262144 | tf_op jit(solution)/shard_map/all_to_all | solution.py:38
  7.9 9.1 %fusion.19 = (bf16[2048,1,128]{2,1,0:T(2,128)(2,1)}, bf16[2048,1,128]{2,1,0:T(2,128)(2,1)}, bf16[2048,1,128]{2,1,0:T(2,128)(2,1)}, bf16[2048,1,128]{2,1,0:T(2,128)(2,1)}) fusion(bf16[2048,4,128]{2,1,0:T(4,128)(2,1)} %param.11), kind=kLoop, calls=%fused_computation.62 | loop fusion | bytes 4194304 | tf_op jit(solution)/shard_map/slice | solution.py:48
  17.3 0.6 select_reduce_fusion
  18.0 0.2 convert_reduce_fusion.4
  18.2 4.5 %fusion.20 = (bf16[2048,1,128]{2,1,0:T(2,128)(2,1)}, bf16[2048,1,128]{2,1,0:T(2,128)(2,1)}, bf16[2048,1,128]{2,1,0:T(2,128)(2,1)}, bf16[2048,1,128]{2,1,0:T(2,128)(2,1)}) fusion(bf16[2048,4,128]{2,1,0:T(4,128)(2,1)S(1)} %copy-done.3), kind=kLoop, calls=%fused_computation.63 | loop fusion | bytes 4194304 | tf_op jit(solution)/shard_map/slice | solution.py:48
  22.8 1.6 %fusion.24 = (f32[128]{0:T(128)S(1)}, f32[128,2048]{1,0:T(8,128)S(1)}) fusion(bf16[2048,1,128]{2,1,0:T(2,128)(2,1)} %get-tuple-element.11, bf16[16,4,8,128]{3,2,1,0:T(8,128)(2,1)S(1)} %bitcast.98), kind=kOutput, calls=%fused_computation.67 | convolution fusion | flops 67633024 | bytes 1606144 | tf_op jit(solution)/shard_map/dot_general | solution.py:10
  24.5 0.3 convert_reduce_fusion.3
  24.9 1.6 %fusion.23 = (f32[128]{0:T(128)S(1)}, f32[128,2048]{1,0:T(8,128)S(1)}) fusion(bf16[2048,1,128]{2,1,0:T(2,128)(2,1)} %get-tuple-element.13, bf16[16,4,8,128]{3,2,1,0:T(8,128)(2,1)S(1)} %bitcast.99), kind=kOutput, calls=%fused_computation.66 | convolution fusion | flops 67633024 | bytes 1606144 | tf_op jit(solution)/shard_map/dot_general | solution.py:10
  26.6 0.3 convert_reduce_fusion.2
  27.0 2.6 %fusion.22 = (f32[128]{0:T(128)S(1)}, f32[128,2048]{1,0:T(8,128)}) fusion(bf16[2048,1,128]{2,1,0:T(2,128)(2,1)} %get-tuple-element.12, bf16[16,4,8,128]{3,2,1,0:T(8,128)(2,1)S(1)} %bitcast.100), kind=kOutput, calls=%fused_computation.65 | convolution fusion | flops 67633024 | bytes 1606144 | tf_op jit(solution)/shard_map/dot_general | solution.py:10
  29.6 1.5 %convert_reduce_fusion.1 = f32[128]{0:T(128)S(1)} fusion(f32[128,2048]{1,0:T(8,128)} %get-tuple-element.22, f32[128]{0:T(128)S(1)} %get-tuple-element.21), kind=kLoop, calls=%fused_computation.16 | loop fusion | flops 1048448 | bytes 1049600 | tf_op jit(solution)/shard_map/reduce_sum | solution.py:17
  31.2 2.6 %fusion.21 = (f32[128]{0:T(128)S(1)}, f32[128,2048]{1,0:T(8,128)}) fusion(bf16[2048,1,128]{2,1,0:T(2,128)(2,1)} %get-tuple-element.14, bf16[16,4,8,128]{3,2,1,0:T(8,128)(2,1)S(1)} %bitcast.101), kind=kOutput, calls=%fused_computation.64 | convolution fusion | flops 67633024 | bytes 1606144 | tf_op jit(solution)/shard_map/dot_general | solution.py:10
  33.8 1.5 %convert_reduce_fusion = f32[128]{0:T(128)S(1)} fusion(f32[128,2048]{1,0:T(8,128)} %get-tuple-element.20, f32[128]{0:T(128)S(1)} %get-tuple-element.19), kind=kLoop, calls=%fused_computation.15 | loop fusion | flops 1048448 | bytes 1049600 | tf_op jit(solution)/shard_map/reduce_sum | solution.py:17
  35.6 0.7 reshape.114
  36.3 5.1 %all-to-all-start.3 = ((f32[4,1,128]{2,1,0:T(1,128)}), f32[4,1,128]{2,1,0:T(1,128)S(1)}, u32[]{:S(2)}, u32[]{:S(2)}) async-start(f32[4,1,128]{2,1,0:T(1,128)} %reshape.114), calls=%async_computation.3 | async-start | bytes 4096 | tf_op jit(solution)/shard_map/all_to_all | solution.py:107
  41.4 1.7 %convolution_bitcast_fusion.3 = f32[16,1,8,128]{3,2,0,1:T(8,128)S(1)} fusion(bf16[2048,1,128]{2,1,0:T(2,128)(2,1)} %get-tuple-element.15, f32[128,2048]{1,0:T(8,128)S(1)} %get-tuple-element.26, f32[128]{0:T(128)S(1)} %get-tuple-element.25), kind=kOutput, calls=%fused_computation.8 | convolution fusion | flops 67633152 | bytes 1638912 | tf_op jit(solution)/shard_map/dot_general | solution.py:18
  43.1 1.6 %convolution_bitcast_fusion.2 = f32[16,1,8,128]{3,2,0,1:T(8,128)S(1)} fusion(bf16[2048,1,128]{2,1,0:T(2,128)(2,1)} %get-tuple-element.17, f32[128,2048]{1,0:T(8,128)S(1)} %get-tuple-element.24, f32[128]{0:T(128)S(1)} %get-tuple-element.23), kind=kOutput, calls=%fused_computation.7 | convolution fusion | flops 67633152 | bytes 1638912 | tf_op jit(solution)/shard_map/dot_general | solution.py:18
  44.7 0.3 convolution_bitcast_fusion.1
  45.1 0.3 convolution_bitcast_fusion
  45.6 0.7 reshape.112
  46.2 0.6 all-to-all-done.3
  46.8 4.5 %all-to-all-start.1 = ((f32[4,1,128]{2,1,0:T(1,128)}), f32[4,1,128]{2,1,0:T(1,128)S(1)}, u32[]{:S(2)}, u32[]{:S(2)}) async-start(f32[4,1,128]{2,1,0:T(1,128)} %reshape.112), calls=%async_computation.1 | async-start | bytes 4096 | tf_op jit(solution)/shard_map/all_to_all | solution.py:104
  51.4 0.7 %copy.26 = f32[16,4,8,128]{3,2,1,0:T(8,128)} copy(f32[16,4,8,128]{3,2,0,1:T(8,128)S(1)} %pad_maximum_fusion) | data formatting | bytes 524288 | tf_op jit(solution)/shard_map/stack | solution.py:55
  52.1 0.5 broadcast.28
  52.6 0.7 reduce
  53.3 3.4 %all-to-all-done.1 = f32[4,1,128]{2,1,0:T(1,128)S(1)} async-done(((f32[4,1,128]{2,1,0:T(1,128)}), f32[4,1,128]{2,1,0:T(1,128)S(1)}, u32[]{:S(2)}, u32[]{:S(2)}) %all-to-all-start.1) | async-done | bytes 2080 | tf_op jit(solution)/shard_map/all_to_all | solution.py:104
  56.8 3.4 %all-to-all-start.2 = ((f32[4,4,32,128]{3,2,1,0:T(8,128)}), f32[4,4,32,128]{3,2,1,0:T(8,128)S(1)}, u32[]{:S(2)}, u32[]{:S(2)}) async-start(f32[4,4,32,128]{3,2,1,0:T(8,128)} %bitcast.30), calls=%async_computation.2 | async-start | bytes 524288 | tf_op jit(solution)/shard_map/all_to_all | solution.py:97
  60.2 0.7 reduce.1
  61.0 5.9 %all-to-all-done.2 = f32[4,4,32,128]{3,2,1,0:T(8,128)S(1)} async-done(((f32[4,4,32,128]{3,2,1,0:T(8,128)}), f32[4,4,32,128]{3,2,1,0:T(8,128)S(1)}, u32[]{:S(2)}, u32[]{:S(2)}) %all-to-all-start.2) | async-done | bytes 262176 | tf_op jit(solution)/shard_map/all_to_all | solution.py:97
  66.9 0.1 multiply_reduce_fusion
  67.1 1.0 %fusion.4 = bf16[4,32,128]{2,1,0:T(8,128)(2,1)} fusion(f32[4,32,128]{2,1,0:T(8,128)S(1)} %multiply_reduce_fusion, bf16[4,192,4,128]{3,2,1,0:T(4,128)(2,1)S(1)} %copy-done.8, f32[4,32]{1,0:T(4,128)S(1)} %get-tuple-element.5, f32[4,32]{1,0:T(4,128)S(1)} %get-tuple-element.6, f32[4,4,128]{2,1,0:T(4,128)S(1)} %convert_element_type.46, ...), kind=kOutput, calls=%fused_computation.14 | convolution fusion | flops 6488064 | bytes 994048 | tf_op jit(solution)/shard_map/bgqs,bsgd->bgqd/dot_general | solution.py:81
  (52 shorter events, 1.6 us)
Async XLA Ops:
  0.0 17.3 %copy-start = (bf16[4,192,4,128]{3,2,1,0:T(4,128)(2,1)S(1)}, bf16[4,192,4,128]{3,2,1,0:T(4,128)(2,1)}, u32[]{:S(2)}) copy-start(bf16[4,192,4,128]{3,2,1,0:T(4,128)(2,1)} %param.13) | copy-start | bytes 2359300
  1.5 21.3 %all-to-all-start = ((bf16[4,4,32,128]{3,2,1,0:T(8,128)(2,1)}), bf16[4,4,32,128]{3,2,1,0:T(8,128)(2,1)S(1)}, u32[]{:S(2)}, u32[]{:S(2)}) async-start(bf16[4,4,32,128]{3,2,1,0:T(8,128)(2,1)} %stack.16), calls=%async_computation | async-start | bytes 262144 | tf_op jit(solution)/shard_map/all_to_all | solution.py:38
  7.9 9.2 %copy-start.6 = (bf16[4,32,128]{2,1,0:T(8,128)(2,1)S(1)}, bf16[4,32,128]{2,1,0:T(8,128)(2,1)}, u32[]{:S(2)}) copy-start(bf16[4,32,128]{2,1,0:T(8,128)(2,1)} %param.8) | copy-start | bytes 98308
  7.9 9.2 %copy-start.9 = (bf16[4,4,128]{2,1,0:T(4,128)(2,1)S(1)}, bf16[4,4,128]{2,1,0:T(4,128)(2,1)}, u32[]{:S(2)}) copy-start(bf16[4,4,128]{2,1,0:T(4,128)(2,1)} %param.9) | copy-start | bytes 12292
  7.9 9.3 %copy-start.10 = (s32[4]{0:T(128)S(1)}, s32[4]{0:T(128)}, u32[]{:S(2)}) copy-start(s32[4]{0:T(128)} %param.15) | copy-start | bytes 52
  7.9 10.3 %copy-start.3 = (bf16[2048,4,128]{2,1,0:T(4,128)(2,1)S(1)}, bf16[2048,4,128]{2,1,0:T(4,128)(2,1)}, u32[]{:S(2)}) copy-start(bf16[2048,4,128]{2,1,0:T(4,128)(2,1)} %param.12) | copy-start | bytes 6291460
  18.2 4.6 %copy-start.7 = (bf16[4,4,128]{2,1,0:T(4,128)(2,1)S(1)}, bf16[4,4,128]{2,1,0:T(4,128)(2,1)}, u32[]{:S(2)}) copy-start(bf16[4,4,128]{2,1,0:T(4,128)(2,1)} %param.10) | copy-start | bytes 12292
  36.3 10.6 %all-to-all-start.3 = ((f32[4,1,128]{2,1,0:T(1,128)}), f32[4,1,128]{2,1,0:T(1,128)S(1)}, u32[]{:S(2)}, u32[]{:S(2)}) async-start(f32[4,1,128]{2,1,0:T(1,128)} %reshape.114), calls=%async_computation.3 | async-start | bytes 4096 | tf_op jit(solution)/shard_map/all_to_all | solution.py:107
  41.3 3.3 %copy-start.1 = (f32[128,2048]{1,0:T(8,128)S(1)}, f32[128,2048]{1,0:T(8,128)}, u32[]{:S(2)}) copy-start(f32[128,2048]{1,0:T(8,128)} %get-tuple-element.22) | copy-start | bytes 3145732
  41.3 3.3 %copy-start.5 = (bf16[2048,1,128]{2,1,0:T(2,128)(2,1)S(1)}, bf16[2048,1,128]{2,1,0:T(2,128)(2,1)}, u32[]{:S(2)}) copy-start(bf16[2048,1,128]{2,1,0:T(2,128)(2,1)} %get-tuple-element.16) | copy-start | bytes 1572868
  41.3 3.7 %copy-start.2 = (f32[128,2048]{1,0:T(8,128)S(1)}, f32[128,2048]{1,0:T(8,128)}, u32[]{:S(2)}) copy-start(f32[128,2048]{1,0:T(8,128)} %get-tuple-element.20) | copy-start | bytes 3145732
  41.4 3.7 %copy-start.4 = (bf16[2048,1,128]{2,1,0:T(2,128)(2,1)S(1)}, bf16[2048,1,128]{2,1,0:T(2,128)(2,1)}, u32[]{:S(2)}) copy-start(bf16[2048,1,128]{2,1,0:T(2,128)(2,1)} %get-tuple-element.18) | copy-start | bytes 1572868
  45.1 22.0 %copy-start.8 = (bf16[4,192,4,128]{3,2,1,0:T(4,128)(2,1)S(1)}, bf16[4,192,4,128]{3,2,1,0:T(4,128)(2,1)}, u32[]{:S(2)}) copy-start(bf16[4,192,4,128]{3,2,1,0:T(4,128)(2,1)} %param.14) | copy-start | bytes 2359300
  46.8 9.9 %all-to-all-start.1 = ((f32[4,1,128]{2,1,0:T(1,128)}), f32[4,1,128]{2,1,0:T(1,128)S(1)}, u32[]{:S(2)}, u32[]{:S(2)}) async-start(f32[4,1,128]{2,1,0:T(1,128)} %reshape.112), calls=%async_computation.1 | async-start | bytes 4096 | tf_op jit(solution)/shard_map/all_to_all | solution.py:104
  56.8 10.2 %all-to-all-start.2 = ((f32[4,4,32,128]{3,2,1,0:T(8,128)}), f32[4,4,32,128]{3,2,1,0:T(8,128)S(1)}, u32[]{:S(2)}, u32[]{:S(2)}) async-start(f32[4,4,32,128]{3,2,1,0:T(8,128)} %bitcast.30), calls=%async_computation.2 | async-start | bytes 524288 | tf_op jit(solution)/shard_map/all_to_all | solution.py:97
